TPU v7x, 32 devices: a whole 2x2x4 slice. The times are simulated.
32 devices in a mesh: ep: 4 (over z), fsdp: 8 (over y, x, core).
Axes of the slice: x: 2, y: 2, z: 4, core: 2. Of those that a mesh axis runs over, the one named last changes fastest.
Arguments:
- train_gate: float32 [64, 2048, 1408], P('ep', 'fsdp'), may hold values from -0.1875 to 0.1875
- train_up: float32 [64, 2048, 1408], P('ep', 'fsdp'), may hold values from -0.1875 to 0.1875
- train_down: float32 [64, 1408, 2048], P('ep', None, 'fsdp'), may hold values from -0.21875 to 0.21875
- router_weight: float32 [2048, 64], P('fsdp', 'ep'), may hold values from -0.125 to 0.125
- router_gain: float32 [2048], P('fsdp'), may hold values from 0.25 to 1.75
Outputs:
- ready_gate: bfloat16 [64, 2048, 1408], P('ep', None, 'fsdp')
- ready_up: bfloat16 [64, 2048, 1408], P('ep', None, 'fsdp')
- ready_down: bfloat16 [64, 1408, 2048], P('ep', 'fsdp')
- scale_gate: float32 [64, 1408], P('ep', 'fsdp')
- scale_up: float32 [64, 1408], P('ep', 'fsdp')
- scale_down: float32 [64, 1408], P('ep', 'fsdp')
- serve_router: bfloat16 [2048, 64], replicated
All inputs are finite; a program needn't handle non-finite values. Where the computation divides by a largest or mean magnitude, that divisor is 1e-20 or more.
Results may differ from a plain program's by a relative error of at most 0.012.
Values may be sent and summed in bfloat16 or wider, within the bound.
A program may use at most 192 MiB of HBM per device.

v0:
```python
import jax
import jax.numpy as jnp
from jax import lax
from jax.sharding import PartitionSpec as P

D_MODEL = 2048


def shards(train_gate, train_up, train_down, router_weight, router_gain):
    total_gate, total_up, total_down = (
        lax.psum(jnp.sum(jnp.abs(train_gate), axis=1).astype(jnp.bfloat16), "fsdp").astype(
            jnp.float32
        ),
        lax.psum(jnp.sum(jnp.abs(train_up), axis=1).astype(jnp.bfloat16), "fsdp").astype(
            jnp.float32
        ),
        lax.psum(jnp.sum(jnp.abs(train_down), axis=2).astype(jnp.bfloat16), "fsdp").astype(
            jnp.float32
        ),
    )
    scale_gate = total_gate / D_MODEL
    scale_up = total_up / D_MODEL
    scale_down = total_down / D_MODEL
    narrow_gate, narrow_up, narrow_down = (
        (train_gate / jnp.expand_dims(scale_gate, 1)).astype(jnp.bfloat16),
        (train_up / jnp.expand_dims(scale_up, 1)).astype(jnp.bfloat16),
        (train_down / jnp.expand_dims(scale_down, 2)).astype(jnp.bfloat16),
    )
    ready_gate, ready_up = (
        lax.all_to_all(narrow_gate, "fsdp", split_axis=2, concat_axis=1, tiled=True),
        lax.all_to_all(narrow_up, "fsdp", split_axis=2, concat_axis=1, tiled=True),
    )
    ready_down = lax.all_to_all(narrow_down, "fsdp", split_axis=1, concat_axis=2, tiled=True)
    scale_gate = lax.dynamic_slice_in_dim(
        scale_gate, lax.axis_index("fsdp") * ready_gate.shape[2], ready_gate.shape[2], axis=1
    )
    scale_up = lax.dynamic_slice_in_dim(
        scale_up, lax.axis_index("fsdp") * ready_up.shape[2], ready_up.shape[2], axis=1
    )
    scale_down = lax.dynamic_slice_in_dim(
        scale_down, lax.axis_index("fsdp") * ready_down.shape[1], ready_down.shape[1], axis=1
    )
    part_router = (router_weight * router_gain[:, None]).astype(jnp.bfloat16)
    row_router = lax.all_gather(part_router, "fsdp", axis=0, tiled=True)
    serve_router = lax.all_gather(row_router, "ep", axis=1, tiled=True)
    return (ready_gate, ready_up, ready_down, scale_gate, scale_up, scale_down, serve_router)


def solution(mesh):
    in_specs = (
        P("ep", "fsdp", None),
        P("ep", "fsdp", None),
        P("ep", None, "fsdp"),
        P("fsdp", "ep"),
        P("fsdp"),
    )
    out_specs = (
        P("ep", None, "fsdp"),
        P("ep", None, "fsdp"),
        P("ep", "fsdp", None),
        P("ep", "fsdp"),
        P("ep", "fsdp"),
        P("ep", "fsdp"),
        P(),
    )
    return jax.shard_map(shards, mesh=mesh, in_specs=in_specs, out_specs=out_specs, check_vma=False)
```

profile of v0, /device:TPU:0, one launch (start us, length us, event | category | flops | bytes accessed | tf_op | source)
XLA Modules:
  0.0 617.4 jit_solution(11987987628351158617)
XLA Ops:
  7.2 9.2 %abs_reduce_fusion = bf16[16,1408]{1,0:T(8,128)(2,1)} fusion(f32[16,1408,256]{2,1,0:T(8,128)} %param.7), kind=kLoop, calls=%fused_computation.2 | loop fusion | flops 11511808 | bytes 23113728 | tf_op jit(solution)/shard_map/reduce_sum | solution.py:17
  16.4 5.0 copy-done
  21.4 11.7 %abs_reduce_fusion.1 = (bf16[16,1408]{1,0:T(8,128)(2,1)}, bf16[16,1408]{1,0:T(8,128)(2,1)}) fusion(f32[16,256,1408]{2,1,0:T(8,128)S(1)} %copy-done, f32[16,256,1408]{2,1,0:T(8,128)} %param.5), kind=kLoop, calls=%fused_computation.4 | loop fusion | flops 23023616 | bytes 46227456 | tf_op jit(solution)/shard_map/reduce_sum | solution.py:14
  33.1 23.7 %copy.28 = f32[16,256,1408]{1,0,2:T(8,128)} copy(f32[16,256,1408]{2,1,0:T(8,128)} %param.6) | data formatting | bytes 46137344 | tf_op args[1]
  56.8 31.4 %all-reduce.3.cloned.1.call-done = (bf16[16,1408]{1,0:T(8,128)(2,1)}, bf16[16,1408]{1,0:T(8,128)(2,1)}, bf16[16,1408]{1,0:T(8,128)(2,1)}) async-done(((bf16[16,1408]{1,0:T(8,128)(2,1)}, bf16[16,1408]{1,0:T(8,128)(2,1)}, bf16[16,1408]{1,0:T(8,128)(2,1)}), (bf16[16,1408]{1,0:T(8,128)(2,1)}, bf16[16,1408]{1,0:T(8,128)(2,1)}, bf16[16,1408]{1,0:T(8,128)(2,1)})) %all-reduce.3.cloned.1.call-update) | async-done | bytes 135184 | tf_op jit(solution)/shard_map/psum | solution.py:11
  88.3 0.8 convert_multiply_fusion.1
  89.3 14.2 %divide_convert_fusion = bf16[16,256,1408]{1,0,2:T(8,128)(2,1)} fusion(f32[16,256,1408]{1,0,2:T(8,128)} %copy.28, f32[16,1408]{0,1:T(8,128)S(1)} %copy.27), kind=kLoop, calls=%fused_computation.3 | loop fusion | flops 11534336 | bytes 34693120 | tf_op jit(solution)/shard_map/convert_element_type | solution.py:26
  103.5 5.2 all-to-all-start.1
  108.8 23.7 %copy.24 = f32[16,256,1408]{1,0,2:T(8,128)} copy(f32[16,256,1408]{2,1,0:T(8,128)} %param.5) | data formatting | bytes 46137344 | tf_op args[0]
  132.8 14.2 %divide_convert_fusion.1 = bf16[16,256,1408]{1,0,2:T(8,128)(2,1)} fusion(f32[16,256,1408]{1,0,2:T(8,128)} %copy.24, f32[16,1408]{0,1:T(8,128)S(1)} %copy.23), kind=kLoop, calls=%fused_computation.5 | loop fusion | flops 11534336 | bytes 34693120 | tf_op jit(solution)/shard_map/convert_element_type | solution.py:25
  147.0 89.5 %all-to-all-done.1 = bf16[16,256,1408]{1,0,2:T(8,128)(2,1)} async-done(((bf16[16,256,1408]{1,0,2:T(8,128)(2,1)}), bf16[16,256,1408]{1,0,2:T(8,128)(2,1)}, u32[]{:S(2)}, u32[]{:S(2)}) %all-to-all-start.1) | async-done | bytes 11534368 | tf_op jit(solution)/shard_map/all_to_all | solution.py:31
  236.5 5.3 all-to-all-start
  242.1 32.6 %fusion = bf16[16,1408,256]{2,0,1:T(8,128)(2,1)} fusion(f32[16,1408,256]{2,1,0:T(8,128)} %param.7, f32[16,1408]{0,1:T(8,128)S(1)} %copy.31), kind=kLoop, calls=%fused_computation.1 | loop fusion | flops 11534336 | bytes 34693120 | tf_op jit(solution)/shard_map/convert_element_type | solution.py:27
  274.7 94.8 %all-to-all-done = bf16[16,256,1408]{1,0,2:T(8,128)(2,1)} async-done(((bf16[16,256,1408]{1,0,2:T(8,128)(2,1)}), bf16[16,256,1408]{1,0,2:T(8,128)(2,1)}, u32[]{:S(2)}, u32[]{:S(2)}) %all-to-all-start) | async-done | bytes 11534368 | tf_op jit(solution)/shard_map/all_to_all | solution.py:30
  369.6 5.3 all-to-all-start.2
  374.9 130.9 %all_gather.6 = bf16[2048,16]{0,1:T(8,128)(2,1)S(1)} all-gather(bf16[256,16]{0,1:T(8,128)(2,1)S(1)} %multiply_convert_fusion), channel_id=1, replica_groups=mesh['ep'=4,'fsdp'=8] {'fsdp'}, dimensions={0}, use_global_device_ids=true | all-gather | bytes 73728 | tf_op jit(solution)/shard_map/all_gather | solution.py:44
  505.8 14.2 %all_gather.7 = bf16[2048,64]{0,1:T(8,128)(2,1)S(1)} all-gather(bf16[2048,16]{0,1:T(8,128)(2,1)S(1)} %all_gather.6), channel_id=1, replica_groups=mesh['ep'=4,'fsdp'=8] {'ep'}, dimensions={1}, use_global_device_ids=true | all-gather | bytes 327680 | tf_op jit(solution)/shard_map/all_gather | solution.py:45
  522.0 11.3 %copy.30 = bf16[16,8,256,176]{2,1,3,0:T(8,128)(2,1)} copy(bf16[16,8,256,176]{2,0,3,1:T(8,128)(2,1)} %bitcast.5) | data formatting | bytes 23068672 | tf_op jit(solution)/shard_map/all_to_all | solution.py:31
  533.3 18.0 %all_to_all.46 = bf16[16,2048,176]{1,2,0:T(8,128)(2,1)} reshape(bf16[16,8,256,176]{2,1,3,0:T(8,128)(2,1)} %copy.30) | data formatting | bytes 23068672 | tf_op jit(solution)/shard_map/all_to_all | solution.py:31
  551.3 11.3 %copy.26 = bf16[16,8,256,176]{2,1,3,0:T(8,128)(2,1)} copy(bf16[16,8,256,176]{2,0,3,1:T(8,128)(2,1)} %bitcast.2) | data formatting | bytes 23068672 | tf_op jit(solution)/shard_map/all_to_all | solution.py:30
  562.6 18.0 %all_to_all.42 = bf16[16,2048,176]{1,2,0:T(8,128)(2,1)} reshape(bf16[16,8,256,176]{2,1,3,0:T(8,128)(2,1)} %copy.26) | data formatting | bytes 23068672 | tf_op jit(solution)/shard_map/all_to_all | solution.py:30
  580.6 11.3 %copy.33 = bf16[16,176,8,256]{3,2,1,0:T(8,128)(2,1)} copy(bf16[16,176,8,256]{3,0,1,2:T(8,128)(2,1)} %bitcast.7) | data formatting | bytes 23068672 | tf_op jit(solution)/shard_map/all_to_all | solution.py:33
  591.9 18.0 %all_to_all.50 = bf16[16,176,2048]{2,1,0:T(8,128)(2,1)} reshape(bf16[16,176,8,256]{3,2,1,0:T(8,128)(2,1)} %copy.33) | data formatting | bytes 23068672 | tf_op jit(solution)/shard_map/all_to_all | solution.py:33
  609.9 0.7 copy.43
  (21 shorter events, 2.9 us)
Async XLA Ops:
  7.2 81.1 %all-reduce.3.cloned.1.call-start = ((), (), s32[]{:S(2)}) async-start(), calls=%async_computation.3 | async-start | bytes 270336 | tf_op jit(solution)/shard_map/psum | solution.py:11
  7.2 14.2 %copy-start = (f32[16,256,1408]{2,1,0:T(8,128)S(1)}, f32[16,256,1408]{2,1,0:T(8,128)}, u32[]{:S(2)}) copy-start(f32[16,256,1408]{2,1,0:T(8,128)} %param.6) | copy-start | bytes 69206016
  103.5 133.0 %all-to-all-start.1 = ((bf16[16,256,1408]{1,0,2:T(8,128)(2,1)}), bf16[16,256,1408]{1,0,2:T(8,128)(2,1)}, u32[]{:S(2)}, u32[]{:S(2)}) async-start(bf16[16,256,1408]{1,0,2:T(8,128)(2,1)} %divide_convert_fusion), calls=%async_computation.1 | async-start | bytes 23068672 | tf_op jit(solution)/shard_map/all_to_all | solution.py:31
  108.8 23.7 %copy-start.2 = (bf16[16,1408]{1,0:T(8,128)(2,1)S(1)}, bf16[16,1408]{1,0:T(8,128)(2,1)}, u32[]{:S(2)}) copy-start(bf16[16,1408]{1,0:T(8,128)(2,1)} %get-tuple-element.7) | copy-start | bytes 135172
  132.8 109.0 %copy-start.1 = (bf16[16,1408]{1,0:T(8,128)(2,1)S(1)}, bf16[16,1408]{1,0:T(8,128)(2,1)}, u32[]{:S(2)}) copy-start(bf16[16,1408]{1,0:T(8,128)(2,1)} %get-tuple-element.9) | copy-start | bytes 135172
  236.5 133.0 %all-to-all-start = ((bf16[16,256,1408]{1,0,2:T(8,128)(2,1)}), bf16[16,256,1408]{1,0,2:T(8,128)(2,1)}, u32[]{:S(2)}, u32[]{:S(2)}) async-start(bf16[16,256,1408]{1,0,2:T(8,128)(2,1)} %divide_convert_fusion.1), calls=%async_computation | async-start | bytes 23068672 | tf_op jit(solution)/shard_map/all_to_all | solution.py:30
  242.1 132.7 %copy-start.3 = (f32[256,16]{0,1:T(8,128)S(1)}, f32[256,16]{0,1:T(8,128)}, u32[]{:S(2)}) copy-start(f32[256,16]{0,1:T(8,128)} %param.8) | copy-start | bytes 49156
  242.1 132.7 %copy-start.4 = (f32[256]{0:T(256)S(1)}, f32[256]{0:T(256)}, u32[]{:S(2)}) copy-start(f32[256]{0:T(256)} %param.9) | copy-start | bytes 3076
  369.6 211.0 %all-to-all-start.2 = ((bf16[16,1408,256]{2,0,1:T(8,128)(2,1)}), bf16[16,1408,256]{2,0,1:T(8,128)(2,1)}, u32[]{:S(2)}, u32[]{:S(2)}) async-start(bf16[16,1408,256]{2,0,1:T(8,128)(2,1)} %fusion), calls=%async_computation.2 | async-start | bytes 23068672 | tf_op jit(solution)/shard_map/all_to_all | solution.py:33
Sparse Core Ops, SparseCore 0:
  33.2 54.9 all-reduce.2
where the time goes:
time: 620 us; the launch traced here: 617 us
  waiting for transfers between devices  216 us (35%)
  blocking collectives  145 us (23%)
  local copies, waits for them, and re-layouts  144 us (23%)
  other arithmetic  82.7 us (13%)
  starting transfers between devices  15.8 us (3%)
  between operations  14.2 us (2%)
    all_gather x1, blocking collectives, shards(): row_router = lax.all_gather(part_router, 'fsdp', axis=0, tiled=True)  131 us
    all_to_all x1, waiting for transfers between devices, shards(): lax.all_to_all(narrow_gate, 'fsdp', split_axis=2, concat_axis=1, tiled=True)  94.8 us
    all_to_all x1, waiting for transfers between devices, shards(): lax.all_to_all(narrow_up, 'fsdp', split_axis=2, concat_axis=1, tiled=True)  89.5 us
    unnamed x13, local copies, waits for them, and re-layouts  53.1 us
    convert_element_type x1, other arithmetic, shards(): (train_down / jnp.expand_dims(scale_down, 2)).astype(jnp.bfloat16)  32.6 us
    psum x1, waiting for transfers between devices, shards(): lax.psum(jnp.sum(jnp.abs(train_gate), axis=1).astype(jnp.bfloat16), 'fsdp')  31.4 us
    all_to_all x2, local copies, waits for them, and re-layouts, shards(): lax.all_to_all(narrow_gate, 'fsdp', split_axis=2, concat_axis=1, tiled=True)  29.3 us
    all_to_all x2, local copies, waits for them, and re-layouts, shards(): lax.all_to_all(narrow_up, 'fsdp', split_axis=2, concat_axis=1, tiled=True)  29.3 us
  transfers between devices with their start and end apart: 4, of which 3 were waited for; matrix products, arithmetic and copies ran while one was open for 19% of the time, Pallas kernels for 0%

commit v1 on v0

--- a/solution.py
+++ b/solution.py
@@ -30,7 +30,10 @@
         lax.all_to_all(narrow_gate, "fsdp", split_axis=2, concat_axis=1, tiled=True),
         lax.all_to_all(narrow_up, "fsdp", split_axis=2, concat_axis=1, tiled=True),
     )
-    ready_down = lax.all_to_all(narrow_down, "fsdp", split_axis=1, concat_axis=2, tiled=True)
+    size = lax.axis_size("fsdp")
+    parts = jnp.stack(jnp.split(narrow_down, size, axis=1), axis=0)
+    parts = lax.all_to_all(parts, "fsdp", split_axis=0, concat_axis=0)
+    ready_down = jnp.concatenate(parts, axis=2)
     scale_gate = lax.dynamic_slice_in_dim(
         scale_gate, lax.axis_index("fsdp") * ready_gate.shape[2], ready_gate.shape[2], axis=1
     )

time: 620 us -> 600 us (0.968)
  other arithmetic: 82.7 us -> 59.9 us
  waiting for transfers between devices: 216 us -> 229 us
  local copies, waits for them, and re-layouts: 144 us -> 134 us
    all_to_all x2 -> x0, local copies, waits for them, and re-layouts: 29.3 us -> none  [shards(): lax.all_to_all(narrow_down, 'fsdp', split_axis=1, concat_axis=2, tiled=True)]
    convert_element_type x1, other arithmetic: 32.6 us -> 9.8 us  [shards(): (train_down / jnp.expand_dims(scale_down, 2)).astype(jnp.bfloat16)]
    all_to_all x1, waiting for transfers between devices: 89.5 us -> 108 us  [shards(): lax.all_to_all(narrow_up, 'fsdp', split_axis=2, concat_axis=1, tiled=True)]
    reshape x0 -> x1, local copies, waits for them, and re-layouts: none -> 10 us  [shards(): ready_down = jnp.concatenate(parts, axis=2)]
    unnamed x13 -> x20, local copies, waits for them, and re-layouts: 53.1 us -> 61.6 us
  transfers between devices with their start and end apart: 4 -> 4, of which waited for: 3 -> 3; matrix products, arithmetic and copies ran while one was open for 19% -> 18% of each run, Pallas kernels for 0% -> 0%
where the time goes in v1:
time: 600 us; the launch traced here: 598 us
  waiting for transfers between devices  229 us (38%)
  blocking collectives  145 us (24%)
  local copies, waits for them, and re-layouts  134 us (22%)
  other arithmetic  59.9 us (10%)
  starting transfers between devices  15.8 us (3%)
  between operations  14.2 us (2%)
    all_gather x1, blocking collectives, shards(): row_router = lax.all_gather(part_router, 'fsdp', axis=0, tiled=True)  131 us
    all_to_all x1, waiting for transfers between devices, shards(): lax.all_to_all(narrow_up, 'fsdp', split_axis=2, concat_axis=1, tiled=True)  108 us
    all_to_all x1, waiting for transfers between devices, shards(): lax.all_to_all(narrow_gate, 'fsdp', split_axis=2, concat_axis=1, tiled=True)  89.6 us
    unnamed x20, local copies, waits for them, and re-layouts  61.6 us
    psum x1, waiting for transfers between devices, shards(): lax.psum(jnp.sum(jnp.abs(train_gate), axis=1).astype(jnp.bfloat16), 'fsdp')  31.4 us
    all_to_all x2, local copies, waits for them, and re-layouts, shards(): lax.all_to_all(narrow_gate, 'fsdp', split_axis=2, concat_axis=1, tiled=True)  29.3 us
    all_to_all x2, local copies, waits for them, and re-layouts, shards(): lax.all_to_all(narrow_up, 'fsdp', split_axis=2, concat_axis=1, tiled=True)  29.3 us
    convert_element_type x1, other arithmetic, shards(): (train_gate / jnp.expand_dims(scale_gate, 1)).astype(jnp.bfloat16)  14.2 us
  transfers between devices with their start and end apart: 4, of which 3 were waited for; matrix products, arithmetic and copies ran while one was open for 18% of the time, Pallas kernels for 0%

profile of v1, /device:TPU:0, one launch (start us, length us, event | category | flops | bytes accessed | tf_op | source)
XLA Modules:
  0.0 598.0 jit_solution(2541055940146341403)
XLA Ops:
  7.2 9.2 %abs_reduce_fusion = bf16[16,1408]{1,0:T(8,128)(2,1)} fusion(f32[16,1408,256]{2,1,0:T(8,128)} %param.7), kind=kLoop, calls=%fused_computation.1 | loop fusion | flops 11511808 | bytes 23113728 | tf_op jit(solution)/shard_map/reduce_sum | solution.py:17
  16.4 5.0 copy-done
  21.4 11.7 %abs_reduce_fusion.1 = (bf16[16,1408]{1,0:T(8,128)(2,1)}, bf16[16,1408]{1,0:T(8,128)(2,1)}) fusion(f32[16,256,1408]{2,1,0:T(8,128)} %param.6, f32[16,256,1408]{2,1,0:T(8,128)S(1)} %copy-done), kind=kLoop, calls=%fused_computation.3 | loop fusion | flops 23023616 | bytes 46227456 | tf_op jit(solution)/shard_map/reduce_sum | solution.py:14
  33.1 23.7 %copy.24 = f32[16,256,1408]{1,0,2:T(8,128)} copy(f32[16,256,1408]{2,1,0:T(8,128)} %param.5) | data formatting | bytes 46137344 | tf_op args[0]
  56.8 31.4 %all-reduce.3.cloned.1.call-done = (bf16[16,1408]{1,0:T(8,128)(2,1)}, bf16[16,1408]{1,0:T(8,128)(2,1)}, bf16[16,1408]{1,0:T(8,128)(2,1)}) async-done(((bf16[16,1408]{1,0:T(8,128)(2,1)}, bf16[16,1408]{1,0:T(8,128)(2,1)}, bf16[16,1408]{1,0:T(8,128)(2,1)}), (bf16[16,1408]{1,0:T(8,128)(2,1)}, bf16[16,1408]{1,0:T(8,128)(2,1)}, bf16[16,1408]{1,0:T(8,128)(2,1)})) %all-reduce.3.cloned.1.call-update) | async-done | bytes 135184 | tf_op jit(solution)/shard_map/psum | solution.py:11
  89.3 14.2 %divide_convert_fusion.2 = bf16[16,256,1408]{1,0,2:T(8,128)(2,1)} fusion(f32[16,256,1408]{1,0,2:T(8,128)} %copy.24, f32[16,1408]{0,1:T(8,128)S(1)} %copy.23), kind=kLoop, calls=%fused_computation.4 | loop fusion | flops 11534336 | bytes 34693120 | tf_op jit(solution)/shard_map/convert_element_type | solution.py:25
  103.6 5.2 all-to-all-start
  108.8 23.7 %copy.28 = f32[16,256,1408]{1,0,2:T(8,128)} copy(f32[16,256,1408]{2,1,0:T(8,128)} %param.6) | data formatting | bytes 46137344 | tf_op args[1]
  132.8 14.2 %divide_convert_fusion.1 = bf16[16,256,1408]{1,0,2:T(8,128)(2,1)} fusion(f32[16,256,1408]{1,0,2:T(8,128)} %copy.28, f32[16,1408]{0,1:T(8,128)S(1)} %copy.27), kind=kLoop, calls=%fused_computation.2 | loop fusion | flops 11534336 | bytes 34693120 | tf_op jit(solution)/shard_map/convert_element_type | solution.py:26
  147.0 89.6 %all-to-all-done = bf16[16,256,1408]{1,0,2:T(8,128)(2,1)} async-done(((bf16[16,256,1408]{1,0,2:T(8,128)(2,1)}), bf16[16,256,1408]{1,0,2:T(8,128)(2,1)}, u32[]{:S(2)}, u32[]{:S(2)}) %all-to-all-start) | async-done | bytes 11534368 | tf_op jit(solution)/shard_map/all_to_all | solution.py:30
  236.6 5.3 all-to-all-start.1
  241.9 9.8 %divide_convert_fusion = bf16[16,1408,256]{2,1,0:T(8,128)(2,1)S(1)} fusion(f32[16,1408,256]{2,1,0:T(8,128)} %param.7, f32[16,1408]{1,0:T(8,128)S(1)} %convert_multiply_fusion), kind=kLoop, calls=%fused_computation | loop fusion | flops 11534336 | bytes 34693120 | tf_op jit(solution)/shard_map/convert_element_type | solution.py:27
  252.8 1.2 fusion.6
  257.6 1.2 fusion.2
  258.9 1.2 fusion.1
  261.3 108.3 %all-to-all-done.1 = bf16[16,256,1408]{1,0,2:T(8,128)(2,1)} async-done(((bf16[16,256,1408]{1,0,2:T(8,128)(2,1)}), bf16[16,256,1408]{1,0,2:T(8,128)(2,1)}, u32[]{:S(2)}, u32[]{:S(2)}) %all-to-all-start.1) | async-done | bytes 11534368 | tf_op jit(solution)/shard_map/all_to_all | solution.py:31
  369.6 5.3 all-to-all-start.2
  374.9 130.9 %all_gather.6 = bf16[2048,16]{0,1:T(8,128)(2,1)S(1)} all-gather(bf16[256,16]{0,1:T(8,128)(2,1)S(1)} %multiply_convert_fusion), channel_id=1, replica_groups=mesh['ep'=4,'fsdp'=8] {'fsdp'}, dimensions={0}, use_global_device_ids=true | all-gather | bytes 73728 | tf_op jit(solution)/shard_map/all_gather | solution.py:47
  505.8 14.0 %all_gather.7 = bf16[2048,64]{0,1:T(8,128)(2,1)S(1)} all-gather(bf16[2048,16]{0,1:T(8,128)(2,1)S(1)} %all_gather.6), channel_id=1, replica_groups=mesh['ep'=4,'fsdp'=8] {'ep'}, dimensions={1}, use_global_device_ids=true | all-gather | bytes 327680 | tf_op jit(solution)/shard_map/all_gather | solution.py:48
  521.8 11.3 %copy.26 = bf16[16,8,256,176]{2,1,3,0:T(8,128)(2,1)} copy(bf16[16,8,256,176]{2,0,3,1:T(8,128)(2,1)} %bitcast.2) | data formatting | bytes 23068672 | tf_op jit(solution)/shard_map/all_to_all | solution.py:30
  533.1 18.0 %all_to_all.32 = bf16[16,2048,176]{1,2,0:T(8,128)(2,1)} reshape(bf16[16,8,256,176]{2,1,3,0:T(8,128)(2,1)} %copy.26) | data formatting | bytes 23068672 | tf_op jit(solution)/shard_map/all_to_all | solution.py:30
  551.1 11.3 %copy.30 = bf16[16,8,256,176]{2,1,3,0:T(8,128)(2,1)} copy(bf16[16,8,256,176]{2,0,3,1:T(8,128)(2,1)} %bitcast.5) | data formatting | bytes 23068672 | tf_op jit(solution)/shard_map/all_to_all | solution.py:31
  562.4 18.0 %all_to_all.36 = bf16[16,2048,176]{1,2,0:T(8,128)(2,1)} reshape(bf16[16,8,256,176]{2,1,3,0:T(8,128)(2,1)} %copy.30) | data formatting | bytes 23068672 | tf_op jit(solution)/shard_map/all_to_all | solution.py:31
  580.4 10.0 %copy.34 = bf16[8,16,22,8,256]{4,3,0,2,1:T(8,128)(2,1)} copy(bf16[8,16,22,8,256]{4,3,2,1,0:T(8,128)(2,1)} %bitcast.15) | data formatting | bytes 23068672 | tf_op jit(solution)/shard_map/reshape | solution.py:36
  (27 shorter events, 10.1 us)
Async XLA Ops:
  7.2 81.1 %all-reduce.3.cloned.1.call-start = ((), (), s32[]{:S(2)}) async-start(), calls=%async_computation.3 | async-start | bytes 270336 | tf_op jit(solution)/shard_map/psum | solution.py:11
  7.2 14.2 %copy-start = (f32[16,256,1408]{2,1,0:T(8,128)S(1)}, f32[16,256,1408]{2,1,0:T(8,128)}, u32[]{:S(2)}) copy-start(f32[16,256,1408]{2,1,0:T(8,128)} %param.5) | copy-start | bytes 69206016
  103.6 133.0 %all-to-all-start = ((bf16[16,256,1408]{1,0,2:T(8,128)(2,1)}), bf16[16,256,1408]{1,0,2:T(8,128)(2,1)}, u32[]{:S(2)}, u32[]{:S(2)}) async-start(bf16[16,256,1408]{1,0,2:T(8,128)(2,1)} %divide_convert_fusion.2), calls=%async_computation | async-start | bytes 23068672 | tf_op jit(solution)/shard_map/all_to_all | solution.py:30
  108.8 23.7 %copy-start.2 = (bf16[16,1408]{1,0:T(8,128)(2,1)S(1)}, bf16[16,1408]{1,0:T(8,128)(2,1)}, u32[]{:S(2)}) copy-start(bf16[16,1408]{1,0:T(8,128)(2,1)} %get-tuple-element.8) | copy-start | bytes 135172
  147.0 94.8 %copy-start.1 = (bf16[16,1408]{1,0:T(8,128)(2,1)S(1)}, bf16[16,1408]{1,0:T(8,128)(2,1)}, u32[]{:S(2)}) copy-start(bf16[16,1408]{1,0:T(8,128)(2,1)} %get-tuple-element.9) | copy-start | bytes 135172
  236.6 133.0 %all-to-all-start.1 = ((bf16[16,256,1408]{1,0,2:T(8,128)(2,1)}), bf16[16,256,1408]{1,0,2:T(8,128)(2,1)}, u32[]{:S(2)}, u32[]{:S(2)}) async-start(bf16[16,256,1408]{1,0,2:T(8,128)(2,1)} %divide_convert_fusion.1), calls=%async_computation.1 | async-start | bytes 23068672 | tf_op jit(solution)/shard_map/all_to_all | solution.py:31
  261.3 113.6 %copy-start.3 = (f32[256,16]{0,1:T(8,128)S(1)}, f32[256,16]{0,1:T(8,128)}, u32[]{:S(2)}) copy-start(f32[256,16]{0,1:T(8,128)} %param.8) | copy-start | bytes 49156
  261.3 113.6 %copy-start.4 = (f32[256]{0:T(256)S(1)}, f32[256]{0:T(256)}, u32[]{:S(2)}) copy-start(f32[256]{0:T(256)} %param.9) | copy-start | bytes 3076
  369.6 210.8 %all-to-all-start.2 = ((bf16[8,16,176,256]{3,2,1,0:T(8,128)(2,1)}), bf16[8,16,176,256]{3,2,1,0:T(8,128)(2,1)}, u32[]{:S(2)}, u32[]{:S(2)}) async-start(bf16[8,16,176,256]{3,2,1,0:T(8,128)(2,1)} %fusion), calls=%async_computation.2 | async-start | bytes 23068672 | tf_op jit(solution)/shard_map/all_to_all | solution.py:35
Sparse Core Ops, SparseCore 0:
  33.3 54.9 all-reduce.2
